TPU v7x, 256 devices: a whole 4x4x8 slice. The times are simulated.
256 devices in a mesh: row: 8 (over x, y_lo), col: 32 (over z, y_hi, core).
Axes of the slice: x: 4, y: 4 (y_hi: 2, y_lo: 2; y = y_hi * 2 + y_lo), z: 8, core: 2. Of those that a mesh axis runs over, the one named last changes fastest.
Arguments:
- grad_out: bfloat16 [2048, 8192], P('col', 'row'), may hold values from -6 to 6
- weight: bfloat16 [28672, 8192], P('col', 'row'), may hold values from -0.0625 to 0.0625
Outputs:
- grad_in: bfloat16 [2048, 28672], P('row', 'col')
All inputs are finite; a program needn't handle non-finite values.
Results may differ from a plain program's by a relative error of at most 0.001.
Values may be sent and summed in bfloat16 or wider, within the bound.
A program may use at most 64 MiB of HBM per device.

v0:
```python
import jax
import jax.numpy as jnp
from jax import lax
from jax.sharding import Mesh
from jax.sharding import PartitionSpec as P

ROW = ("row_0", "row_1")


def scatter_axes(array, axes, dim):
    if not axes:
        return array
    nearer = lax.psum_scatter(array, axes[0], scatter_dimension=dim, tiled=True)
    return scatter_axes(nearer, axes[1:], dim)


def contract(rows_block, weight):
    return lax.dot_general(
        rows_block, weight, (((1,), (1,)), ((), ())), preferred_element_type=jnp.float32
    )


def local(grad_out, weight):
    partial_value = contract(lax.all_gather(grad_out, "col", axis=0, tiled=True), weight)
    return scatter_axes(partial_value, ROW, 0).astype(jnp.bfloat16)


def solution(mesh):
    finer = Mesh(mesh.devices.reshape(4, 2, mesh.shape["col"]), ("row_0", "row_1", "col"))
    in_specs = (P("col", ROW), P("col", ROW))
    out_specs = P(ROW, "col")
    return jax.shard_map(local, mesh=finer, in_specs=in_specs, out_specs=out_specs, check_vma=False)
```

profile of v0, /device:TPU:1, one launch (start us, length us, event | category | flops | bytes accessed | tf_op | source)
XLA Modules:
  0.0 226.0 jit_solution(12876038008683448927)
XLA Ops:
  6.5 0.0 copy-start
  6.5 0.0 all-gather.2.cloned.1.call-start
  6.5 0.7 all-gather.2.cloned.1.call-update
  7.3 0.0 reduce-scatter.3.cloned.1.call-start
  7.3 93.6 %all-gather.2.cloned.1.call-done = bf16[2048,1024]{1,0:T(8,128)(2,1)} async-done(((bf16[64,1024]{1,0:T(8,128)(2,1)}), bf16[2048,1024]{1,0:T(8,128)(2,1)}) %all-gather.2.cloned.1.call-update) | async-done | bytes 4194320 | tf_op jit(solution)/shard_map/all_gather | solution.py:24
  100.9 0.0 copy-done
  100.9 8.8 %fusion = f32[2048,896]{1,0:T(8,128)} fusion(bf16[2048,1024]{1,0:T(8,128)(2,1)} %all-gather.2.cloned.1.call-done, bf16[896,1024]{1,0:T(8,128)(2,1)S(1)} %copy-done), kind=kOutput, calls=%fused_computation | convolution fusion | flops 3758096384 | bytes 13369344 | tf_op jit(solution)/shard_map/dot_general | solution.py:18
  109.7 0.0 reduce-scatter.3.cloned.1.call-update
  109.7 0.0 reduce-scatter.5.cloned.1.call-start
  109.7 71.4 %reduce-scatter.3.cloned.1.call-done = f32[512,896]{1,0:T(8,128)} async-done(((f32[2048,896]{1,0:T(8,128)}), f32[512,896]{1,0:T(8,128)}) %reduce-scatter.3.cloned.1.call-update) | async-done | bytes 1835024 | tf_op jit(solution)/shard_map/reduce_scatter | solution.py:13
  181.2 0.0 reduce-scatter.5.cloned.1.call-update
  181.2 36.3 %reduce-scatter.5.cloned.1.call-done = f32[256,896]{1,0:T(8,128)} async-done(((f32[512,896]{1,0:T(8,128)}), f32[256,896]{1,0:T(8,128)}) %reduce-scatter.5.cloned.1.call-update) | async-done | bytes 917520 | tf_op jit(solution)/shard_map/reduce_scatter | solution.py:13
  217.5 2.0 convert_element_type.3
Async XLA Ops:
  6.5 94.4 %copy-start = (bf16[896,1024]{1,0:T(8,128)(2,1)S(1)}, bf16[896,1024]{1,0:T(8,128)(2,1)}, u32[]{:S(2)}) copy-start(bf16[896,1024]{1,0:T(8,128)(2,1)} %param.3) | copy-start | bytes 5505028
  6.5 94.4 %all-gather.2.cloned.1.call-start = ((), (), s32[]{:S(2)}) async-start(), calls=%async_computation.2 | async-start | bytes 4325376 | tf_op jit(solution)/shard_map/all_gather | solution.py:24
  7.3 173.9 %reduce-scatter.3.cloned.1.call-start = ((), (), s32[]{:S(2)}) async-start(), calls=%async_computation.3 | async-start | bytes 9175040 | tf_op jit(solution)/shard_map/reduce_scatter | solution.py:13
  109.7 107.8 %reduce-scatter.5.cloned.1.call-start = ((), (), s32[]{:S(2)}) async-start(), calls=%async_computation.4 | async-start | bytes 2752512 | tf_op jit(solution)/shard_map/reduce_scatter | solution.py:13
Sparse Core Ops, SparseCore 0:
  10.1 90.7 all-gather.1
  109.8 71.3 reduce-scatter.2
  183.7 33.7 reduce-scatter.4
where the time goes:
time: 226 us
  waiting for transfers between devices  202 us (89%)
  between operations  13.1 us (6%)
  matrix products  8.75 us (4%)
    reduce_scatter x2, waiting for transfers between devices, scatter_axes(): nearer = lax.psum_scatter(array, axes[0], scatter_dimension=dim, tiled=True)  108 us
    all_gather x1, waiting for transfers between devices, local(): lax.all_gather(grad_out, 'col', axis=0, tiled=True)  93.6 us
    dot_general x1, matrix products, contract(): lax.dot_general(rows_block, weight, (((1,), (1,)), ((), ())), preferred_e...  8.75 us
  transfers between devices with their start and end apart: 3, of which 3 were waited for; matrix products, arithmetic and copies ran while one was open for 0% of the time, Pallas kernels for 0%

commit v1 on v0

v1 whole, which is shorter than its diff:
```python
import jax
import jax.numpy as jnp
from jax import lax
from jax.experimental import pallas as pl
from jax.experimental.pallas import tpu as pltpu
from jax.sharding import PartitionSpec as P

MESH = pl.DeviceIdType.MESH
CH = 128
L_REL = (0, 1, 1, 0)
H_REL = (0, 0, 1, 1)
NT = (((1,), (1,)), ((), ()))


def kernel(
    g_ref, w_ref, o_ref, gbuf, wn, cbuf, relay, farin, nearin,
    s1s, s1r, zs, zr, ps, pr, ws, wr, fs, fr, ds, dr, rs, rr,
):
    n_ch = w_ref.shape[0] // CH
    tb, feat = g_ref.shape
    blk = 4 * tb
    half = blk // 2
    row = lax.axis_index("row")
    col = lax.axis_index("col")
    x = lax.div(row, 2)
    lo = lax.rem(row, 2)
    z = lax.div(col, 4)
    hi = lax.rem(lax.div(col, 2), 2)
    c = lax.rem(col, 2)
    is_src = lax.rem(z, 2) == lo

    def dev(x=x, lo=lo, z=z, hi=hi, c=c):
        return (x * 2 + lo, z * 4 + hi * 2 + c)

    zn = (lax.rem(z + 1, 8), lax.rem(z + 7, 8))
    xn = (lax.rem(x + 1, 4), lax.rem(x + 3, 4))
    partner = dev(c=1 - c)
    z_dev = (dev(z=zn[0]), dev(z=zn[1]))
    x_dev = (dev(x=xn[0]), dev(x=xn[1]))
    w_dev = dev(lo=1 - lo)
    h_dev = dev(hi=1 - hi)
    wh_dev = dev(lo=1 - lo, hi=1 - hi)

    barrier = pltpu.get_barrier_semaphore()
    peers = (partner, *z_dev, *x_dev, w_dev, h_dev, wh_dev)
    for peer in peers:
        pl.semaphore_signal(barrier, inc=1, device_id=peer, device_id_type=MESH)
    pl.semaphore_wait(barrier, len(peers))

    def rc(src, dst, ss, sr, to):
        return pltpu.make_async_remote_copy(
            src_ref=src, dst_ref=dst, send_sem=ss, recv_sem=sr, device_id=to, device_id_type=MESH
        )

    def block(slot, k, core):
        h = hi if H_REL[k] == 0 else 1 - hi
        at = pl.multiple_of(slot * blk + (h * 2 + core) * tb, tb)
        return gbuf.at[L_REL[k], pl.ds(at, tb), :]

    def place(slot, l, h, core):
        at = pl.multiple_of(slot * blk + (h * 2 + core) * tb, tb)
        return gbuf.at[l, pl.ds(at, tb), :]

    def slot_of(shift):
        return lax.div(lax.rem(z + shift, 8), 2)

    s0 = lax.div(z, 2)

    def pidx(d, r, k):
        return 4 + d * 8 + r * 4 + k

    @pl.when(is_src)
    def _():
        own = place(s0, 0, hi, c)
        rc(g_ref, place(s0, 0, hi, c), s1s.at[0], s1r.at[2], h_dev).start()
        for d in range(2):
            rc(g_ref, own, zs.at[d, 0, 0], zr.at[d, 0, 0], z_dev[d]).start()
        rc(g_ref, own, ps.at[0], pr.at[0], partner).start()

    @pl.when(jnp.logical_not(is_src))
    def _():
        rc(g_ref, place(s0, 1, hi, c), s1s.at[0], s1r.at[0], w_dev).start()
        rc(g_ref, place(s0, 1, hi, c), s1s.at[1], s1r.at[1], wh_dev).start()

    def w_copy(j):
        at = pl.ds(pl.multiple_of(j * CH, CH), CH)
        return rc(w_ref.at[at, :], wn.at[at, :], ws.at[j], wr.at[j], w_dev)

    for j in range(n_ch):
        w_copy(j).start()

    def relay_to(slot, k, d, out_r, send_r):
        b = block(slot, k, c)
        rc(b, b, zs.at[d, send_r, k], zr.at[d, out_r, k], z_dev[d]).start()

    def share(slot, k, i):
        b = block(slot, k, c)
        rc(b, b, ps.at[i], pr.at[i], partner).start()

    def arrived(slot, k, d, r):
        b = block(slot, k, c)
        rc(b, b, zs.at[d, r, k], zr.at[d, r, k], z_dev[d]).wait_recv()

    @pl.when(is_src)
    def _():
        gbuf[0, pl.ds(pl.multiple_of(s0 * blk + (hi * 2 + c) * tb, tb), tb), :] = g_ref[...]
        for k in range(1, 4):
            b = block(s0, k, c)
            rc(b, b, s1s.at[0], s1r.at[k - 1], h_dev).wait_recv()
            for d in range(2):
                relay_to(s0, k, d, 0, 0)
            share(s0, k, k)
        near = (slot_of(6), slot_of(2))
        for k in range(4):
            for d in range(2):
                arrived(near[d], k, d, 0)
                relay_to(near[d], k, d, 1, 1)
                share(near[d], k, pidx(d, 0, k))
        opp = slot_of(4)
        for i in range(2):
            for d in range(2):
                k = d * 2 + i
                arrived(opp, k, d, 1)
                share(opp, k, pidx(d, 1, k))
        for k in range(4):
            b = block(s0, k, 1 - c)
            rc(b, b, ps.at[k], pr.at[k], partner).wait_recv()
            for d in range(2):
                b = block(near[d], k, 1 - c)
                i = pidx(d, 0, k)
                rc(b, b, ps.at[i], pr.at[i], partner).wait_recv()
        for d in range(2):
            for i in range(2):
                k = d * 2 + i
                b = block(opp, k, 1 - c)
                i = pidx(d, 1, k)
                rc(b, b, ps.at[i], pr.at[i], partner).wait_recv()

    @pl.when(jnp.logical_not(is_src))
    def _():
        near = (slot_of(7), slot_of(1))
        far = (slot_of(5), slot_of(3))
        for k in range(4):
            for d in range(2):
                arrived(near[d], k, d, 0)
                relay_to(near[d], k, d, 0, 0)
                share(near[d], k, pidx(d, 0, k))
        for k in (0, 2, 1, 3):
            for d in range(2):
                arrived(far[d], k, d, 1)
                if k // 2 == d:
                    relay_to(far[d], k, d, 1, 1)
                share(far[d], k, pidx(d, 1, k))
        for r, slots in ((0, near), (1, far)):
            for k in range(4):
                for d in range(2):
                    b = block(slots[d], k, 1 - c)
                    i = pidx(d, r, k)
                    rc(b, b, ps.at[i], pr.at[i], partner).wait_recv()

    far_slot = lax.rem(x + 2, 4)

    def far_copy(j, d):
        src = cbuf.at[j, pl.ds(pl.multiple_of(far_slot * blk + d * half, half), half), :]
        return rc(src, farin.at[d, j], fs.at[d, j], fr.at[d, j], x_dev[d])

    def direct_copy(j, d):
        at = (1 - d) * half
        src = cbuf.at[j, pl.ds(pl.multiple_of(xn[d] * blk + at, half), half), :]
        return rc(src, nearin.at[d, j, pl.ds(at, half), :], ds.at[d, j], dr.at[d, j], x_dev[d])

    def relay_copy(j, d):
        dst = nearin.at[d, j, pl.ds(d * half, half), :]
        return rc(relay.at[d, j], dst, rs.at[d, j], rr.at[d, j], x_dev[d])

    def step(j, _):
        @pl.when(j < n_ch)
        def _():
            w_copy(j).wait_recv()
            at = pl.ds(pl.multiple_of(j * CH, CH), CH)

            def compute(slot):
                rows = pl.ds(pl.multiple_of(slot * blk, blk), blk)
                total = lax.dot_general(gbuf[0, rows, :], w_ref[at, :], NT, preferred_element_type=jnp.float32)
                total += lax.dot_general(gbuf[1, rows, :], wn[at, :], NT, preferred_element_type=jnp.float32)
                cbuf[j, rows, :] = total

            compute(far_slot)
            for d in range(2):
                far_copy(j, d).start()
            for d in range(2):
                compute(xn[d])
                direct_copy(j, d).start()
            compute(x)

        @pl.when(jnp.logical_and(j >= 1, j <= n_ch))
        def _():
            i = j - 1
            for d in range(2):
                far_copy(i, d).wait_recv()
                rows = pl.ds(pl.multiple_of(xn[d] * blk + d * half, half), half)
                relay[d, i] = cbuf[i, rows, :] + farin[d, i]
                relay_copy(i, d).start()

        @pl.when(j >= 2)
        def _():
            i = j - 2
            for d in range(2):
                direct_copy(i, d).wait_recv()
                relay_copy(i, d).wait_recv()
            rows = pl.ds(pl.multiple_of(x * blk, blk), blk)
            total = cbuf[i, rows, :] + nearin[0, i] + nearin[1, i]
            o_ref[:, pl.ds(pl.multiple_of(i * CH, CH), CH)] = total.astype(o_ref.dtype)

        return 0

    lax.fori_loop(0, n_ch + 2, step, 0)

    def drain(j, _):
        w_copy(j).wait_send()
        for d in range(2):
            far_copy(j, d).wait_send()
            direct_copy(j, d).wait_send()
            relay_copy(j, d).wait_send()
        return 0

    lax.fori_loop(0, n_ch, drain, 0)

    def sent(sem):
        rc(g_ref, g_ref, sem, sem, partner).wait_send()

    sent(s1s.at[0])
    for d in range(2):
        for k in range(4):
            sent(zs.at[d, 0, k])
            sent(ps.at[pidx(d, 0, k)])
            if k // 2 == d:
                sent(zs.at[d, 1, k])
                sent(ps.at[pidx(d, 1, k)])

    @pl.when(is_src)
    def _():
        for k in range(4):
            sent(ps.at[k])
        for d in range(2):
            for k in range(4):
                if k // 2 != d:
                    sent(zs.at[d, 1, k])

    @pl.when(jnp.logical_not(is_src))
    def _():
        sent(s1s.at[1])
        for d in range(2):
            for k in range(4):
                if k // 2 != d:
                    sent(ps.at[pidx(d, 1, k)])


def local(grad_out, weight):
    tb, feat = grad_out.shape
    hidden = weight.shape[0]
    n_ch = hidden // CH
    blk = 4 * tb
    dma = pltpu.SemaphoreType.DMA
    vmem = pl.BlockSpec(memory_space=pltpu.VMEM)
    return pl.pallas_call(
        kernel,
        out_shape=jax.ShapeDtypeStruct((blk, hidden), jnp.bfloat16),
        in_specs=[vmem, vmem],
        out_specs=vmem,
        scratch_shapes=[
            pltpu.VMEM((2, 4 * blk, feat), jnp.bfloat16),
            pltpu.VMEM((hidden, feat), jnp.bfloat16),
            pltpu.VMEM((n_ch, 4 * blk, CH), jnp.float32),
            pltpu.VMEM((2, n_ch, blk // 2, CH), jnp.float32),
            pltpu.VMEM((2, n_ch, blk // 2, CH), jnp.float32),
            pltpu.VMEM((2, n_ch, blk, CH), jnp.float32),
            dma((2,)), dma((3,)),
            dma((2, 2, 4)), dma((2, 2, 4)),
            dma((20,)), dma((20,)),
            dma((n_ch,)), dma((n_ch,)),
            dma((2, n_ch)), dma((2, n_ch)),
            dma((2, n_ch)), dma((2, n_ch)),
            dma((2, n_ch)), dma((2, n_ch)),
        ],
        compiler_params=pltpu.CompilerParams(
            collective_id=0, has_side_effects=True, vmem_limit_bytes=48 * 1024 * 1024
        ),
    )(grad_out, weight)


def solution(mesh):
    spec = P("col", "row")
    return jax.shard_map(local, mesh=mesh, in_specs=(spec, spec), out_specs=P("row", "col"), check_vma=False)
```

time: 226 us -> 78.6 us (0.35)
  waiting for transfers between devices: 202 us -> 0 us
  Pallas kernels: 0 us -> 75.3 us
  between operations: 13.1 us -> 0.01 us
  matrix products: 8.75 us -> 0 us
  local copies, waits for them, and re-layouts: 0.01 us -> 3.17 us
    reduce_scatter x2 -> x0, waiting for transfers between devices: 108 us -> none  [scatter_axes(): nearer = lax.psum_scatter(array, axes[0], scatter_dimension=dim, tiled=True)]
    all_gather x1 -> x0, waiting for transfers between devices: 93.6 us -> none  [local(): lax.all_gather(grad_out, 'col', axis=0, tiled=True)]
    pallas_call x0 -> x1, Pallas kernels: none -> 75.3 us  [local(): pl.pallas_call(kernel, out_shape=jax.ShapeDtypeStruct((blk, hidden), jnp....]
    dot_general x1 -> x0, matrix products: 8.75 us -> none  [contract(): lax.dot_general(rows_block, weight, (((1,), (1,)), ((), ())), preferred_e...]
    unnamed x2 -> x5, local copies, waits for them, and re-layouts: 0.01 us -> 3.17 us
  transfers between devices with their start and end apart: 3 -> 0, of which waited for: 3 -> 0; matrix products, arithmetic and copies ran while one was open for 0% -> 0% of each run, Pallas kernels for 0% -> 0%
where the time goes in v1:
time: 78.6 us; the launch traced here: 78.5 us
  Pallas kernels  75.3 us (96%)
  local copies, waits for them, and re-layouts  3.17 us (4%)
    pallas_call x1, Pallas kernels, local(): pl.pallas_call(kernel, out_shape=jax.ShapeDtypeStruct((blk, hidden), jnp....  75.3 us
    unnamed x5, local copies, waits for them, and re-layouts  3.17 us

profile of v1, /device:TPU:1, one launch (start us, length us, event | category | flops | bytes accessed | tf_op | source)
XLA Modules:
  0.0 78.5 jit_solution(13590756236044136262)
XLA Ops:
  0.0 0.0 copy-start
  0.0 1.5 %copy-done = bf16[896,1024]{1,0:T(8,128)(2,1)S(1)} copy-done((bf16[896,1024]{1,0:T(8,128)(2,1)S(1)}, bf16[896,1024]{1,0:T(8,128)(2,1)}, u32[]{:S(2)}) %copy-start) | copy-done | bytes 1835032
  1.5 0.0 copy-start.1
  1.5 0.9 %copy-done.1 = bf16[64,1024]{1,0:T(8,128)(2,1)S(1)} copy-done((bf16[64,1024]{1,0:T(8,128)(2,1)S(1)}, bf16[64,1024]{1,0:T(8,128)(2,1)}, u32[]{:S(2)}) %copy-start.1) | copy-done | bytes 131096
  2.4 75.3 %shard_map.28 = bf16[256,896]{1,0:T(8,128)(2,1)S(1)} custom-call(bf16[64,1024]{1,0:T(8,128)(2,1)S(1)} %copy-done.1, bf16[896,1024]{1,0:T(8,128)(2,1)S(1)} %copy-done), custom_call_target="tpu_custom_call" | custom-call | tf_op jit(solution)/shard_map/pallas_call | solution.py:266
  77.7 0.8 copy.4
Async XLA Ops:
  0.0 1.5 %copy-start = (bf16[896,1024]{1,0:T(8,128)(2,1)S(1)}, bf16[896,1024]{1,0:T(8,128)(2,1)}, u32[]{:S(2)}) copy-start(bf16[896,1024]{1,0:T(8,128)(2,1)} %w_ref.1) | copy-start | bytes 5505028
  1.5 0.9 %copy-start.1 = (bf16[64,1024]{1,0:T(8,128)(2,1)S(1)}, bf16[64,1024]{1,0:T(8,128)(2,1)}, u32[]{:S(2)}) copy-start(bf16[64,1024]{1,0:T(8,128)(2,1)} %g_ref.1) | copy-start | bytes 393220

commit v2 on v1

v2 whole, which is shorter than its diff:
```python
import jax
import jax.numpy as jnp
from jax import lax
from jax.experimental import pallas as pl
from jax.experimental.pallas import tpu as pltpu
from jax.sharding import PartitionSpec as P

MESH = pl.DeviceIdType.MESH
CH = 128
ORDER = (0, 2, 1, 3)
NT = (((1,), (1,)), ((), ()))


def kernel(
    g_hbm, w_hbm, o_ref, g_ref, w_ref, gbuf, wn, cbuf, relay, farin, nearin,
    ls, s1s, s1r, zs, zr, ps, pr, ws, wr, fs, fr, ds, dr, rs, rr,
):
    n_ch = w_ref.shape[0] // CH
    tb, feat = g_ref.shape
    blk = 4 * tb
    half = blk // 2
    n_items = 2 * n_ch
    row = lax.axis_index("row")
    col = lax.axis_index("col")
    x = lax.div(row, 2)
    lo = lax.rem(row, 2)
    z = lax.div(col, 4)
    hi = lax.rem(lax.div(col, 2), 2)
    c = lax.rem(col, 2)
    is_src = lax.rem(z, 2) == lo
    not_src = jnp.logical_not(is_src)

    def dev(x=x, lo=lo, z=z, hi=hi, c=c):
        return (x * 2 + lo, z * 4 + hi * 2 + c)

    zn = (lax.rem(z + 1, 8), lax.rem(z + 7, 8))
    xn = (lax.rem(x + 1, 4), lax.rem(x + 3, 4))
    partner = dev(c=1 - c)
    z_dev = (dev(z=zn[0]), dev(z=zn[1]))
    x_dev = (dev(x=xn[0]), dev(x=xn[1]))
    w_dev = dev(lo=1 - lo)
    h_dev = dev(hi=1 - hi)
    wh_dev = dev(lo=1 - lo, hi=1 - hi)

    barrier = pltpu.get_barrier_semaphore()
    peers = (partner, *z_dev, *x_dev, w_dev, h_dev, wh_dev)
    for peer in peers:
        pl.semaphore_signal(barrier, inc=1, device_id=peer, device_id_type=MESH)
    g_in = pltpu.make_async_copy(g_hbm, g_ref, ls.at[0])
    w_in = pltpu.make_async_copy(w_hbm, w_ref, ls.at[1])
    g_in.start()
    w_in.start()
    g_in.wait()
    w_in.wait()
    pl.semaphore_wait(barrier, len(peers))

    def rc(src, dst, ss, sr, to):
        return pltpu.make_async_remote_copy(
            src_ref=src, dst_ref=dst, send_sem=ss, recv_sem=sr, device_id=to, device_id_type=MESH
        )

    def place(slot, l, h, core):
        at = pl.multiple_of(slot * blk + (h * 2 + core) * tb, tb)
        return gbuf.at[l, pl.ds(at, tb), :]

    def block(slot, k, core):
        return place(slot, lax.rem(lax.div(k + 1, 2), 2), lax.rem(hi + lax.div(k, 2), 2), core)

    def slot_of(shift):
        return lax.div(lax.rem(z + shift, 8), 2)

    s0 = lax.div(z, 2)

    def pidx(d, r, k):
        return 4 + d * 8 + r * 4 + k

    @pl.when(is_src)
    def _():
        own = place(s0, 0, hi, c)
        rc(g_ref, own, s1s.at[0], s1r.at[2], h_dev).start()
        for d in range(2):
            rc(g_ref, own, zs.at[d, 0, 0], zr.at[d, 0, 0], z_dev[d]).start()
        rc(g_ref, own, ps.at[0], pr.at[0], partner).start()

    @pl.when(not_src)
    def _():
        rc(g_ref, place(s0, 1, hi, c), s1s.at[0], s1r.at[0], w_dev).start()
        rc(g_ref, place(s0, 1, hi, c), s1s.at[1], s1r.at[1], wh_dev).start()

    def w_copy(j):
        at = pl.ds(pl.multiple_of(j * CH, CH), CH)
        return rc(w_ref.at[at, :], wn.at[at, :], ws.at[j], wr.at[j], w_dev)

    for j in range(n_ch):
        w_copy(j).start()

    def relay_to(slot, k, d, out_r, send_r):
        b = block(slot, k, c)
        rc(b, b, zs.at[d, send_r, k], zr.at[d, out_r, k], z_dev[d]).start()

    def share(slot, k, i):
        b = block(slot, k, c)
        rc(b, b, ps.at[i], pr.at[i], partner).start()

    def arrived(slot, k, d, r):
        b = block(slot, k, c)
        rc(b, b, zs.at[d, r, k], zr.at[d, r, k], z_dev[d]).wait_recv()

    def shared(slot, k, i):
        b = block(slot, k, 1 - c)
        rc(b, b, ps.at[i], pr.at[i], partner).wait_recv()

    src_near = (slot_of(6), slot_of(2))
    opp = slot_of(4)
    mid_near = (slot_of(7), slot_of(1))
    mid_far = (slot_of(5), slot_of(3))
    early = (jnp.where(is_src, s0, mid_near[0]), jnp.where(is_src, src_near[1], mid_near[1]))
    late = (jnp.where(is_src, src_near[0], mid_far[0]), jnp.where(is_src, opp, mid_far[1]))

    @pl.when(is_src)
    def _():
        gbuf[0, pl.ds(pl.multiple_of(s0 * blk + (hi * 2 + c) * tb, tb), tb), :] = g_ref[...]
        for k in (2, 1, 3):
            b = block(s0, k, c)
            rc(b, b, s1s.at[0], s1r.at[k - 1], h_dev).wait_recv()
            for d in range(2):
                relay_to(s0, k, d, 0, 0)
            share(s0, k, k)
        for k in ORDER:
            for d in range(2):
                arrived(src_near[d], k, d, 0)
                relay_to(src_near[d], k, d, 1, 1)
                share(src_near[d], k, pidx(d, 0, k))
        for k in range(4):
            shared(s0, k, k)
            shared(src_near[1], k, pidx(1, 0, k))

    @pl.when(not_src)
    def _():
        for k in ORDER:
            for d in range(2):
                arrived(mid_near[d], k, d, 0)
                relay_to(mid_near[d], k, d, 0, 0)
                share(mid_near[d], k, pidx(d, 0, k))
        for k in range(4):
            for d in range(2):
                shared(mid_near[d], k, pidx(d, 0, k))

    def gather_step(t):
        @pl.when(jnp.logical_and(not_src, t < 4))
        def _():
            k = 2 * lax.rem(t, 2) + lax.div(t, 2)
            for d in range(2):
                arrived(mid_far[d], k, d, 1)

                @pl.when(lax.rem(t, 2) == d)
                def _():
                    relay_to(mid_far[d], k, d, 1, 1)

                share(mid_far[d], k, pidx(d, 1, k))

        @pl.when(jnp.logical_and(is_src, jnp.logical_and(t >= 2, t < 4)))
        def _():
            for d in range(2):
                k = d * 2 + t - 2
                arrived(opp, k, d, 1)
                share(opp, k, pidx(d, 1, k))

        @pl.when(jnp.logical_and(not_src, t == 4))
        def _():
            for k in range(4):
                for d in range(2):
                    shared(mid_far[d], k, pidx(d, 1, k))

        @pl.when(jnp.logical_and(is_src, t == 4))
        def _():
            for k in range(4):
                shared(src_near[0], k, pidx(0, 0, k))
                shared(opp, k, pidx(k // 2, 1, k))

    def group_of(t):
        u = jnp.maximum(t, 0)
        tail = u >= 8
        e = jnp.where(tail, lax.rem(u, 2), lax.div(u, 4))
        j = jnp.where(tail, lax.div(u, 2), lax.rem(u, 4))
        pair = tuple(jnp.where(e == 0, early[i], late[i]) for i in range(2))
        return e, j, pair

    def inside(slot, pair):
        return jnp.logical_or(slot == pair[0], slot == pair[1])

    far_slot = lax.rem(x + 2, 4)

    def far_copy(j, d):
        src = cbuf.at[j, pl.ds(pl.multiple_of(far_slot * blk + d * half, half), half), :]
        return rc(src, farin.at[d, j], fs.at[d, j], fr.at[d, j], x_dev[d])

    def direct_copy(j, d):
        at = (1 - d) * half
        src = cbuf.at[j, pl.ds(pl.multiple_of(xn[d] * blk + at, half), half), :]
        return rc(src, nearin.at[d, j, pl.ds(at, half), :], ds.at[d, j], dr.at[d, j], x_dev[d])

    def relay_copy(j, d):
        dst = nearin.at[d, j, pl.ds(d * half, half), :]
        return rc(relay.at[d, j], dst, rs.at[d, j], rr.at[d, j], x_dev[d])

    def relay_step(t):
        _, j, pair = group_of(t)
        live = jnp.logical_and(t >= 0, t < n_items)
        for d in range(2):
            @pl.when(jnp.logical_and(live, inside(xn[d], pair)))
            def _():
                far_copy(j, d).wait_recv()
                rows = pl.ds(pl.multiple_of(xn[d] * blk + d * half, half), half)
                relay[d, j] = cbuf[j, rows, :] + farin[d, j]
                relay_copy(j, d).start()

    def final_step(t):
        _, j, pair = group_of(t)

        @pl.when(jnp.logical_and(t >= 0, inside(x, pair)))
        def _():
            for d in range(2):
                direct_copy(j, d).wait_recv()
                relay_copy(j, d).wait_recv()
            rows = pl.ds(pl.multiple_of(x * blk, blk), blk)
            total = cbuf[j, rows, :] + nearin[0, j] + nearin[1, j]
            o_ref[:, pl.ds(pl.multiple_of(j * CH, CH), CH)] = total.astype(o_ref.dtype)

    def compute_step(t):
        e, j, pair = group_of(t)

        @pl.when(t < n_items)
        def _():
            @pl.when(e == 0)
            def _():
                w_copy(j).wait_recv()

            at = pl.ds(pl.multiple_of(j * CH, CH), CH)
            for slot in pair:
                rows = pl.ds(pl.multiple_of(slot * blk, blk), blk)
                total = lax.dot_general(gbuf[0, rows, :], w_ref[at, :], NT, preferred_element_type=jnp.float32)
                total += lax.dot_general(gbuf[1, rows, :], wn[at, :], NT, preferred_element_type=jnp.float32)
                cbuf[j, rows, :] = total

                @pl.when(slot == far_slot)
                def _():
                    for d in range(2):
                        far_copy(j, d).start()

                for d in range(2):
                    @pl.when(slot == xn[d])
                    def _():
                        direct_copy(j, d).start()

    def step(t, _):
        gather_step(t)
        relay_step(t - 2)
        final_step(t - 4)
        compute_step(t)
        return 0

    lax.fori_loop(0, n_items + 4, step, 0)

    def drain(j, _):
        w_copy(j).wait_send()
        for d in range(2):
            far_copy(j, d).wait_send()
            direct_copy(j, d).wait_send()
            relay_copy(j, d).wait_send()
        return 0

    lax.fori_loop(0, n_ch, drain, 0)

    def sent(sem):
        rc(g_ref, g_ref, sem, sem, partner).wait_send()

    sent(s1s.at[0])
    for d in range(2):
        for k in range(4):
            sent(zs.at[d, 0, k])
            sent(ps.at[pidx(d, 0, k)])
            if k // 2 == d:
                sent(zs.at[d, 1, k])
                sent(ps.at[pidx(d, 1, k)])

    @pl.when(is_src)
    def _():
        for k in range(4):
            sent(ps.at[k])
        for d in range(2):
            for k in range(4):
                if k // 2 != d:
                    sent(zs.at[d, 1, k])

    @pl.when(not_src)
    def _():
        sent(s1s.at[1])
        for d in range(2):
            for k in range(4):
                if k // 2 != d:
                    sent(ps.at[pidx(d, 1, k)])


def local(grad_out, weight):
    tb, feat = grad_out.shape
    hidden = weight.shape[0]
    n_ch = hidden // CH
    blk = 4 * tb
    dma = pltpu.SemaphoreType.DMA
    vmem = pl.BlockSpec(memory_space=pltpu.VMEM)
    hbm = pl.BlockSpec(memory_space=pltpu.HBM)
    return pl.pallas_call(
        kernel,
        out_shape=jax.ShapeDtypeStruct((blk, hidden), jnp.bfloat16),
        in_specs=[hbm, hbm],
        out_specs=vmem,
        scratch_shapes=[
            pltpu.VMEM((tb, feat), jnp.bfloat16),
            pltpu.VMEM((hidden, feat), jnp.bfloat16),
            pltpu.VMEM((2, 4 * blk, feat), jnp.bfloat16),
            pltpu.VMEM((hidden, feat), jnp.bfloat16),
            pltpu.VMEM((n_ch, 4 * blk, CH), jnp.float32),
            pltpu.VMEM((2, n_ch, blk // 2, CH), jnp.float32),
            pltpu.VMEM((2, n_ch, blk // 2, CH), jnp.float32),
            pltpu.VMEM((2, n_ch, blk, CH), jnp.float32),
            dma((2,)),
            dma((2,)), dma((3,)),
            dma((2, 2, 4)), dma((2, 2, 4)),
            dma((20,)), dma((20,)),
            dma((n_ch,)), dma((n_ch,)),
            dma((2, n_ch)), dma((2, n_ch)),
            dma((2, n_ch)), dma((2, n_ch)),
            dma((2, n_ch)), dma((2, n_ch)),
        ],
        compiler_params=pltpu.CompilerParams(
            collective_id=0, has_side_effects=True, vmem_limit_bytes=63 * 1024 * 1024
        ),
    )(grad_out, weight)


def solution(mesh):
    spec = P("col", "row")
    return jax.shard_map(local, mesh=mesh, in_specs=(spec, spec), out_specs=P("row", "col"), check_vma=False)
```

time: 78.6 us -> 87.1 us (1.11)
  the two profiles are of different devices: /device:TPU:1 before, /device:TPU:4 now
where the time goes in v2:
time: 87.1 us; the launch traced here: 86.9 us
  Pallas kernels  85.1 us (98%)
  local copies, waits for them, and re-layouts  1.82 us (2%)
    pallas_call x1, Pallas kernels, local(): pl.pallas_call(kernel, out_shape=jax.ShapeDtypeStruct((blk, hidden), jnp....  85.1 us
    unnamed x1, local copies, waits for them, and re-layouts  1.82 us

profile of v2, /device:TPU:4, one launch (start us, length us, event | category | flops | bytes accessed | tf_op | source)
XLA Modules:
  0.0 86.9 jit_solution(2521351421934739332)
XLA Ops:
  0.0 85.1 %shard_map.28 = bf16[256,896]{1,0:T(8,128)(2,1)} custom-call(bf16[64,1024]{1,0:T(8,128)(2,1)} %g_hbm.1, bf16[896,1024]{1,0:T(8,128)(2,1)} %w_hbm.1), custom_call_target="tpu_custom_call" | custom-call | tf_op jit(solution)/shard_map/pallas_call | solution.py:313
  85.1 1.8 %copy.4 = bf16[256,896]{1,0:T(8,128)(2,1)} copy(bf16[256,896]{1,0:T(8,128)(2,1)} %shard_map.28) | data formatting | bytes 917504

commit v3 on v2

--- a/solution.py
+++ b/solution.py
@@ -7,19 +7,22 @@
 
 MESH = pl.DeviceIdType.MESH
 CH = 128
-ORDER = (0, 2, 1, 3)
+ORDER = (0, 1, 3, 2)
+SIDE = (0, 1, 1, 0)
+SPLIT = 8
+LAG = 3
+LAST = 6
 NT = (((1,), (1,)), ((), ()))
 
 
 def kernel(
     g_hbm, w_hbm, o_ref, g_ref, w_ref, gbuf, wn, cbuf, relay, farin, nearin,
-    ls, s1s, s1r, zs, zr, ps, pr, ws, wr, fs, fr, ds, dr, rs, rr,
+    ls, s1s, s1r, zs, zr, ps, pr, ws, wr, fs, fr, ds, dr,
 ):
     n_ch = w_ref.shape[0] // CH
     tb, feat = g_ref.shape
     blk = 4 * tb
     half = blk // 2
-    n_items = 2 * n_ch
     row = lax.axis_index("row")
     col = lax.axis_index("col")
     x = lax.div(row, 2)
@@ -63,8 +66,11 @@
         at = pl.multiple_of(slot * blk + (h * 2 + core) * tb, tb)
         return gbuf.at[l, pl.ds(at, tb), :]
 
+    def side(k):
+        return lax.rem(lax.div(k + 1, 2), 2)
+
     def block(slot, k, core):
-        return place(slot, lax.rem(lax.div(k + 1, 2), 2), lax.rem(hi + lax.div(k, 2), 2), core)
+        return place(slot, side(k), lax.rem(hi + lax.div(k, 2), 2), core)
 
     def slot_of(shift):
         return lax.div(lax.rem(z + shift, 8), 2)
@@ -120,7 +126,7 @@
     @pl.when(is_src)
     def _():
         gbuf[0, pl.ds(pl.multiple_of(s0 * blk + (hi * 2 + c) * tb, tb), tb), :] = g_ref[...]
-        for k in (2, 1, 3):
+        for k in ORDER[1:]:
             b = block(s0, k, c)
             rc(b, b, s1s.at[0], s1r.at[k - 1], h_dev).wait_recv()
             for d in range(2):
@@ -149,11 +155,11 @@
     def gather_step(t):
         @pl.when(jnp.logical_and(not_src, t < 4))
         def _():
-            k = 2 * lax.rem(t, 2) + lax.div(t, 2)
+            k = jnp.where(t < 2, t, 5 - t)
             for d in range(2):
                 arrived(mid_far[d], k, d, 1)
 
-                @pl.when(lax.rem(t, 2) == d)
+                @pl.when(side(k) == d)
                 def _():
                     relay_to(mid_far[d], k, d, 1, 1)
 
@@ -162,7 +168,7 @@
         @pl.when(jnp.logical_and(is_src, jnp.logical_and(t >= 2, t < 4)))
         def _():
             for d in range(2):
-                k = d * 2 + t - 2
+                k = d + (t - 2) * (3 - 2 * d)
                 arrived(opp, k, d, 1)
                 share(opp, k, pidx(d, 1, k))
 
@@ -176,98 +182,118 @@
         def _():
             for k in range(4):
                 shared(src_near[0], k, pidx(0, 0, k))
-                shared(opp, k, pidx(k // 2, 1, k))
+                shared(opp, k, pidx(SIDE[k], 1, k))
+
+    n_items = SPLIT + n_ch - SPLIT // 2
+    flush = n_items - 1
+    far_slot = lax.rem(x + 2, 4)
+    order = (far_slot, xn[0], xn[1], x)
 
     def group_of(t):
-        u = jnp.maximum(t, 0)
-        tail = u >= 8
-        e = jnp.where(tail, lax.rem(u, 2), lax.div(u, 4))
-        j = jnp.where(tail, lax.div(u, 2), lax.rem(u, 4))
-        pair = tuple(jnp.where(e == 0, early[i], late[i]) for i in range(2))
-        return e, j, pair
-
-    def inside(slot, pair):
-        return jnp.logical_or(slot == pair[0], slot == pair[1])
-
-    far_slot = lax.rem(x + 2, 4)
-
-    def far_copy(j, d):
-        src = cbuf.at[j, pl.ds(pl.multiple_of(far_slot * blk + d * half, half), half), :]
-        return rc(src, farin.at[d, j], fs.at[d, j], fr.at[d, j], x_dev[d])
-
-    def direct_copy(j, d):
-        at = (1 - d) * half
-        src = cbuf.at[j, pl.ds(pl.multiple_of(xn[d] * blk + at, half), half), :]
-        return rc(src, nearin.at[d, j, pl.ds(at, half), :], ds.at[d, j], dr.at[d, j], x_dev[d])
-
-    def relay_copy(j, d):
-        dst = nearin.at[d, j, pl.ds(d * half, half), :]
-        return rc(relay.at[d, j], dst, rs.at[d, j], rr.at[d, j], x_dev[d])
-
-    def relay_step(t):
-        _, j, pair = group_of(t)
-        live = jnp.logical_and(t >= 0, t < n_items)
-        for d in range(2):
-            @pl.when(jnp.logical_and(live, inside(xn[d], pair)))
-            def _():
-                far_copy(j, d).wait_recv()
-                rows = pl.ds(pl.multiple_of(xn[d] * blk + d * half, half), half)
-                relay[d, j] = cbuf[j, rows, :] + farin[d, j]
-                relay_copy(j, d).start()
-
-    def final_step(t):
-        _, j, pair = group_of(t)
-
-        @pl.when(jnp.logical_and(t >= 0, inside(x, pair)))
-        def _():
-            for d in range(2):
-                direct_copy(j, d).wait_recv()
-                relay_copy(j, d).wait_recv()
+        full = t >= SPLIT
+        e = lax.div(t, SPLIT // 2)
+        j = jnp.where(full, t - SPLIT // 2, lax.rem(t, SPLIT // 2))
+        pair = tuple(jnp.where(full, order[i], jnp.where(e == 0, early[i], late[i])) for i in range(2))
+        return full, e, j, pair
+
+    def inside(slot, full, pair):
+        return jnp.logical_or(full, jnp.logical_or(slot == pair[0], slot == pair[1]))
+
+    def way(slot, h, full, pair):
+        other = pair[0] + pair[1] - slot
+        return jnp.where(full, h, jnp.where(lax.rem(slot + 1, 4) == other, 0, 1))
+
+    def rows_of(slot, h):
+        return pl.ds(pl.multiple_of(slot * blk + h * half, half), half)
+
+    def far_copy(j, d, h):
+        return rc(cbuf.at[j, rows_of(far_slot, h), :], farin.at[d, j, h], fs.at[j, h], fr.at[d, j, h], x_dev[d])
+
+    def near_dst(j, d, h):
+        return nearin.at[d, j, pl.ds(h * half, half), :]
+
+    def direct_copy(j, d, h):
+        return rc(cbuf.at[j, rows_of(xn[d], h), :], near_dst(j, d, h), ds.at[d, j, h], dr.at[d, j, h], x_dev[d])
+
+    def relay_copy(j, d, h):
+        return rc(relay.at[d, j, h], near_dst(j, d, h), ds.at[d, j, h], dr.at[d, j, h], x_dev[d])
+
+    def relay_step(t, _):
+        full, _, j, pair = group_of(t)
+        for h in range(2):
+            for d in range(2):
+                @pl.when(jnp.logical_and(inside(xn[d], full, pair), way(xn[d], h, full, pair) == d))
+                def _():
+                    far_copy(j, d, h).wait_recv()
+                    relay[d, j, h] = cbuf[j, rows_of(xn[d], h), :] + farin[d, j, h]
+                    relay_copy(j, d, h).start()
+
+        return 0
+
+    def final_step(t, _):
+        full, _, j, pair = group_of(t)
+
+        @pl.when(inside(x, full, pair))
+        def _():
+            for h in range(2):
+                for d in range(2):
+                    direct_copy(j, d, h).wait_recv()
             rows = pl.ds(pl.multiple_of(x * blk, blk), blk)
             total = cbuf[j, rows, :] + nearin[0, j] + nearin[1, j]
             o_ref[:, pl.ds(pl.multiple_of(j * CH, CH), CH)] = total.astype(o_ref.dtype)
 
+        return 0
+
     def compute_step(t):
-        e, j, pair = group_of(t)
-
-        @pl.when(t < n_items)
-        def _():
-            @pl.when(e == 0)
-            def _():
-                w_copy(j).wait_recv()
-
-            at = pl.ds(pl.multiple_of(j * CH, CH), CH)
-            for slot in pair:
-                rows = pl.ds(pl.multiple_of(slot * blk, blk), blk)
-                total = lax.dot_general(gbuf[0, rows, :], w_ref[at, :], NT, preferred_element_type=jnp.float32)
-                total += lax.dot_general(gbuf[1, rows, :], wn[at, :], NT, preferred_element_type=jnp.float32)
-                cbuf[j, rows, :] = total
-
-                @pl.when(slot == far_slot)
-                def _():
-                    for d in range(2):
-                        far_copy(j, d).start()
-
+        full, e, j, pair = group_of(t)
+
+        @pl.when(jnp.logical_or(full, e == 0))
+        def _():
+            w_copy(j).wait_recv()
+
+        at = pl.ds(pl.multiple_of(j * CH, CH), CH)
+
+        def one(i, _):
+            slot = jnp.where(i < 2, jnp.where(i == 0, pair[0], pair[1]), jnp.where(i == 2, order[2], order[3]))
+            rows = pl.ds(pl.multiple_of(slot * blk, blk), blk)
+            total = lax.dot_general(gbuf[0, rows, :], w_ref[at, :], NT, preferred_element_type=jnp.float32)
+            total += lax.dot_general(gbuf[1, rows, :], wn[at, :], NT, preferred_element_type=jnp.float32)
+            cbuf[j, rows, :] = total
+            for h in range(2):
+                to = way(slot, h, full, pair)
                 for d in range(2):
-                    @pl.when(slot == xn[d])
+                    @pl.when(jnp.logical_and(slot == far_slot, to == d))
                     def _():
-                        direct_copy(j, d).start()
+                        far_copy(j, d, h).start()
+
+                    @pl.when(jnp.logical_and(slot == xn[d], to != d))
+                    def _():
+                        direct_copy(j, d, h).start()
+
+            return 0
+
+        lax.fori_loop(0, jnp.where(full, 4, 2), one, 0)
+
+    def relayed(t):
+        return jnp.where(t >= flush, t, jnp.maximum(t - LAG, 0))
 
     def step(t, _):
         gather_step(t)
-        relay_step(t - 2)
-        final_step(t - 4)
+        lax.fori_loop(relayed(t - 1), relayed(t), relay_step, 0)
+        lax.fori_loop(jnp.maximum(t - 1 - LAST, 0), jnp.maximum(t - LAST, 0), final_step, 0)
         compute_step(t)
         return 0
 
-    lax.fori_loop(0, n_items + 4, step, 0)
+    lax.fori_loop(0, n_items, step, 0)
+    lax.fori_loop(n_items - 1, n_items, relay_step, 0)
+    lax.fori_loop(n_items - 1 - LAST, n_items, final_step, 0)
 
     def drain(j, _):
         w_copy(j).wait_send()
-        for d in range(2):
-            far_copy(j, d).wait_send()
-            direct_copy(j, d).wait_send()
-            relay_copy(j, d).wait_send()
+        for h in range(2):
+            far_copy(j, 0, h).wait_send()
+            for d in range(2):
+                direct_copy(j, d, h).wait_send()
         return 0
 
     lax.fori_loop(0, n_ch, drain, 0)
@@ -280,7 +306,7 @@
         for k in range(4):
             sent(zs.at[d, 0, k])
             sent(ps.at[pidx(d, 0, k)])
-            if k // 2 == d:
+            if SIDE[k] == d:
                 sent(zs.at[d, 1, k])
                 sent(ps.at[pidx(d, 1, k)])
 
@@ -290,7 +316,7 @@
             sent(ps.at[k])
         for d in range(2):
             for k in range(4):
-                if k // 2 != d:
+                if SIDE[k] != d:
                     sent(zs.at[d, 1, k])
 
     @pl.when(not_src)
@@ -298,7 +324,7 @@
         sent(s1s.at[1])
         for d in range(2):
             for k in range(4):
-                if k // 2 != d:
+                if SIDE[k] != d:
                     sent(ps.at[pidx(d, 1, k)])
 
 
@@ -321,17 +347,16 @@
             pltpu.VMEM((2, 4 * blk, feat), jnp.bfloat16),
             pltpu.VMEM((hidden, feat), jnp.bfloat16),
             pltpu.VMEM((n_ch, 4 * blk, CH), jnp.float32),
-            pltpu.VMEM((2, n_ch, blk // 2, CH), jnp.float32),
-            pltpu.VMEM((2, n_ch, blk // 2, CH), jnp.float32),
+            pltpu.VMEM((2, n_ch, 2, blk // 2, CH), jnp.float32),
+            pltpu.VMEM((2, n_ch, 2, blk // 2, CH), jnp.float32),
             pltpu.VMEM((2, n_ch, blk, CH), jnp.float32),
             dma((2,)),
             dma((2,)), dma((3,)),
             dma((2, 2, 4)), dma((2, 2, 4)),
             dma((20,)), dma((20,)),
             dma((n_ch,)), dma((n_ch,)),
-            dma((2, n_ch)), dma((2, n_ch)),
-            dma((2, n_ch)), dma((2, n_ch)),
-            dma((2, n_ch)), dma((2, n_ch)),
+            dma((n_ch, 2)), dma((2, n_ch, 2)),
+            dma((2, n_ch, 2)), dma((2, n_ch, 2)),
         ],
         compiler_params=pltpu.CompilerParams(
             collective_id=0, has_side_effects=True, vmem_limit_bytes=63 * 1024 * 1024

time: 87.1 us -> 75.6 us (0.87)
  the two profiles are of different devices: /device:TPU:4 before, /device:TPU:20 now
where the time goes in v3:
time: 75.6 us; the launch traced here: 75.4 us
  Pallas kernels  73.6 us (97%)
  local copies, waits for them, and re-layouts  1.82 us (2%)
    pallas_call x1, Pallas kernels, local(): pl.pallas_call(kernel, out_shape=jax.ShapeDtypeStruct((blk, hidden), jnp....  73.6 us
    unnamed x1, local copies, waits for them, and re-layouts  1.82 us

profile of v3, /device:TPU:20, one launch (start us, length us, event | category | flops | bytes accessed | tf_op | source)
XLA Modules:
  0.0 75.4 jit_solution(18038350745823892942)
XLA Ops:
  0.0 73.6 %shard_map.28 = bf16[256,896]{1,0:T(8,128)(2,1)} custom-call(bf16[64,1024]{1,0:T(8,128)(2,1)} %g_hbm.1, bf16[896,1024]{1,0:T(8,128)(2,1)} %w_hbm.1), custom_call_target="tpu_custom_call" | custom-call | tf_op jit(solution)/shard_map/pallas_call | solution.py:339
  73.6 1.8 %copy.4 = bf16[256,896]{1,0:T(8,128)(2,1)} copy(bf16[256,896]{1,0:T(8,128)(2,1)} %shard_map.28) | data formatting | bytes 917504

commit v4 on v3

v4 whole, which is shorter than its diff:
```python
import jax
import jax.numpy as jnp
from jax import lax
from jax.experimental import pallas as pl
from jax.experimental.pallas import tpu as pltpu
from jax.sharding import PartitionSpec as P

MESH = pl.DeviceIdType.MESH
CH = 128
PARTS = 2
ORDER = ((0, 0), (0, 1), (1, 0), (1, 1), (3, 0), (2, 0), (3, 1), (2, 1))
SIDE = (0, 1, 1, 0)
HALVES = 4
NT = (((1,), (1,)), ((), ()))


def kernel(
    g_hbm, w_hbm, o_ref, g_ref, w_ref, gbuf, wn, cbuf, relay, farin, nearin,
    ls, s1s, s1r, zs, zr, ps, pr, ws, wr, fs, fr, ds, dr, rs, rr,
):
    n_ch = w_ref.shape[0] // CH
    tb, feat = g_ref.shape
    blk = 4 * tb
    half = blk // 2
    row = lax.axis_index("row")
    col = lax.axis_index("col")
    x = lax.div(row, 2)
    lo = lax.rem(row, 2)
    z = lax.div(col, 4)
    hi = lax.rem(lax.div(col, 2), 2)
    c = lax.rem(col, 2)
    is_src = lax.rem(z, 2) == lo
    not_src = jnp.logical_not(is_src)

    def dev(x=x, lo=lo, z=z, hi=hi, c=c):
        return (x * 2 + lo, z * 4 + hi * 2 + c)

    zn = (lax.rem(z + 1, 8), lax.rem(z + 7, 8))
    xn = (lax.rem(x + 1, 4), lax.rem(x + 3, 4))
    partner = dev(c=1 - c)
    z_dev = (dev(z=zn[0]), dev(z=zn[1]))
    x_dev = (dev(x=xn[0]), dev(x=xn[1]))
    w_dev = dev(lo=1 - lo)
    h_dev = dev(hi=1 - hi)
    wh_dev = dev(lo=1 - lo, hi=1 - hi)

    barrier = pltpu.get_barrier_semaphore()
    peers = (partner, *z_dev, *x_dev, w_dev, h_dev, wh_dev)
    for peer in peers:
        pl.semaphore_signal(barrier, inc=1, device_id=peer, device_id_type=MESH)
    g_in = pltpu.make_async_copy(g_hbm, g_ref, ls.at[0])
    w_in = pltpu.make_async_copy(w_hbm, w_ref, ls.at[1])
    g_in.start()
    w_in.start()
    g_in.wait()
    w_in.wait()
    pl.semaphore_wait(barrier, len(peers))

    def rc(src, dst, ss, sr, to):
        return pltpu.make_async_remote_copy(
            src_ref=src, dst_ref=dst, send_sem=ss, recv_sem=sr, device_id=to, device_id_type=MESH
        )

    piece = tb // PARTS

    def place(slot, l, h, core, p):
        at = pl.multiple_of(slot * blk + (h * 2 + core) * tb + p * piece, piece)
        return gbuf.at[l, pl.ds(at, piece), :]

    def side(k):
        return lax.rem(lax.div(k + 1, 2), 2)

    def block(slot, k, core, p):
        return place(slot, side(k), lax.rem(hi + lax.div(k, 2), 2), core, p)

    def slot_of(shift):
        return lax.div(lax.rem(z + shift, 8), 2)

    s0 = lax.div(z, 2)

    def own_part(p):
        return g_ref.at[pl.ds(p * piece, piece), :]

    @pl.when(is_src)
    def _():
        for p in range(PARTS):
            own = place(s0, 0, hi, c, p)
            for d in range(2):
                rc(own_part(p), own, zs.at[d, 0, 0, p], zr.at[d, 0, 0, p], z_dev[d]).start()
            rc(own_part(p), own, s1s.at[0, p], s1r.at[2, p], h_dev).start()
            rc(own_part(p), own, ps.at[0, 0, p], pr.at[0, 0, p], partner).start()

    @pl.when(not_src)
    def _():
        for p in range(PARTS):
            there = place(s0, 1, hi, c, p)
            rc(own_part(p), there, s1s.at[0, p], s1r.at[0, p], w_dev).start()
            rc(own_part(p), there, s1s.at[1, p], s1r.at[1, p], wh_dev).start()

    def w_copy(j):
        at = pl.ds(pl.multiple_of(j * CH, CH), CH)
        return rc(w_ref.at[at, :], wn.at[at, :], ws.at[j], wr.at[j], w_dev)

    for j in range(n_ch):
        w_copy(j).start()

    def relay_to(slot, k, p, d, out_r, send_r):
        b = block(slot, k, c, p)
        rc(b, b, zs.at[d, send_r, k, p], zr.at[d, out_r, k, p], z_dev[d]).start()

    def share(slot, k, p, i):
        b = block(slot, k, c, p)
        rc(b, b, ps.at[i, k, p], pr.at[i, k, p], partner).start()

    def arrived(slot, k, p, d, r):
        b = block(slot, k, c, p)
        rc(b, b, zs.at[d, r, k, p], zr.at[d, r, k, p], z_dev[d]).wait_recv()

    def shared(slot, k, p, i):
        b = block(slot, k, 1 - c, p)
        rc(b, b, ps.at[i, k, p], pr.at[i, k, p], partner).wait_recv()

    def first_of(k, p):
        b = block(s0, k, c, p)
        rc(b, b, s1s.at[0, p], s1r.at[k - 1, p], h_dev).wait_recv()

    src_near = (slot_of(6), slot_of(2))
    opp = slot_of(4)
    mid_near = (slot_of(7), slot_of(1))
    mid_far = (slot_of(5), slot_of(3))
    early = (jnp.where(is_src, s0, mid_near[0]), jnp.where(is_src, src_near[1], mid_near[1]))
    late = (jnp.where(is_src, src_near[0], mid_far[0]), jnp.where(is_src, opp, mid_far[1]))

    def src_near_one(k, p):
        for d in range(2):
            arrived(src_near[d], k, p, d, 0)
            relay_to(src_near[d], k, p, d, 1, 1)
            share(src_near[d], k, p, 1 + d)

    def mid_near_one(k, p):
        for d in range(2):
            arrived(mid_near[d], k, p, d, 0)
            relay_to(mid_near[d], k, p, d, 0, 0)
            share(mid_near[d], k, p, 1 + d)

    def own_one(k, p):
        first_of(k, p)
        for d in range(2):
            relay_to(s0, k, p, d, 0, 0)
        share(s0, k, p, 0)

    def mid_far_one(k, p):
        for d in range(2):
            arrived(mid_far[d], k, p, d, 1)

            @pl.when(side(k) == d)
            def _():
                relay_to(mid_far[d], k, p, d, 1, 1)

            share(mid_far[d], k, p, 3 + d)

    def opp_one(ka, kb, p):
        for d, k in ((0, ka), (1, kb)):
            arrived(opp, k, p, d, 1)
            share(opp, k, p, 3)

    @pl.when(is_src)
    def _():
        gbuf[0, pl.ds(pl.multiple_of(s0 * blk + (hi * 2 + c) * tb, tb), tb), :] = g_ref[...]
        for k, p in ORDER[2:]:
            own_one(k, p)
        for k, p in ORDER:
            src_near_one(k, p)
        for p in range(PARTS):
            opp_one(0, 1, p)

    @pl.when(not_src)
    def _():
        for k, p in ORDER:
            mid_near_one(k, p)
        for k, p in ORDER[:4]:
            mid_far_one(k, p)

    def gather_step(t):
        @pl.when(jnp.logical_and(is_src, t == 3))
        def _():
            for p in range(PARTS):
                opp_one(3, 2, p)

        for p, when in ((0, 0), (1, 1)):
            @pl.when(jnp.logical_and(not_src, t == when))
            def _():
                for i in range(2):
                    mid_far_one(3 - i, p)

    def planes_ready(t):
        for when, ks in ((0, (0, 1)), (HALVES, (3, 2))):
            @pl.when(jnp.logical_and(is_src, t == when))
            def _():
                for k in ks:
                    for p in range(PARTS):
                        shared(s0, k, p, 0)
                        for d in range(2):
                            shared(src_near[d], k, p, 1 + d)
                        shared(opp, k, p, 3)

            @pl.when(jnp.logical_and(not_src, t == when))
            def _():
                for k in ks:
                    for p in range(PARTS):
                        for d in range(2):
                            shared(mid_near[d], k, p, 1 + d)
                            shared(mid_far[d], k, p, 3 + d)

    n_items = HALVES + n_ch
    far_slot = lax.rem(x + 2, 4)
    order = (far_slot, xn[0], xn[1], x)

    def group_of(t):
        full = t >= 2 * HALVES
        j = jnp.where(t < HALVES, t, t - HALVES)
        only = jnp.where(t < HALVES, hi, 1 - hi)
        return full, j, only

    def has(h, full, only):
        return jnp.logical_or(full, only == h)

    def rows_of(slot, h, q):
        return pl.ds(pl.multiple_of(slot * blk + (h * 2 + q) * tb, tb), tb)

    def far_copy(j, d, h):
        return rc(cbuf.at[j, rows_of(far_slot, h, d), :], farin.at[d, j, h], fs.at[d, j, h], fr.at[d, j, h], x_dev[d])

    def near_dst(j, d, h, q):
        return nearin.at[d, j, pl.ds((h * 2 + q) * tb, tb), :]

    def direct_copy(j, d, h):
        src = cbuf.at[j, rows_of(xn[d], h, 1 - d), :]
        return rc(src, near_dst(j, d, h, 1 - d), ds.at[d, j, h], dr.at[d, j, h], x_dev[d])

    def relay_copy(j, d, h):
        return rc(relay.at[d, j, h], near_dst(j, d, h, d), rs.at[d, j, h], rr.at[d, j, h], x_dev[d])

    def relay_step(t, _):
        full, j, only = group_of(t)
        for h in range(2):
            @pl.when(has(h, full, only))
            def _():
                for d in range(2):
                    far_copy(j, d, h).wait_recv()
                    relay[d, j, h] = cbuf[j, rows_of(xn[d], h, d), :] + farin[d, j, h]
                    relay_copy(j, d, h).start()

        return 0

    def final_step(t, _):
        full, j, only = group_of(t)
        for h in range(2):
            @pl.when(has(h, full, only))
            def _():
                for d in range(2):
                    direct_copy(j, d, h).wait_recv()
                    relay_copy(j, d, h).wait_recv()
                rows = pl.ds(h * half, half)
                mine = pl.ds(pl.multiple_of(x * blk + h * half, half), half)
                total = cbuf[j, mine, :] + nearin[0, j, rows, :] + nearin[1, j, rows, :]
                o_ref[rows, pl.ds(pl.multiple_of(j * CH, CH), CH)] = total.astype(o_ref.dtype)

        return 0

    def compute_step(t):
        full, j, only = group_of(t)

        @pl.when(jnp.logical_or(full, t < HALVES))
        def _():
            w_copy(j).wait_recv()

        at = pl.ds(pl.multiple_of(j * CH, CH), CH)

        def product(rows):
            total = lax.dot_general(gbuf[0, rows, :], w_ref[at, :], NT, preferred_element_type=jnp.float32)
            total += lax.dot_general(gbuf[1, rows, :], wn[at, :], NT, preferred_element_type=jnp.float32)
            cbuf[j, rows, :] = total

        def one(i, _):
            slot = jnp.where(i < 2, jnp.where(i == 0, order[0], order[1]), jnp.where(i == 2, order[2], order[3]))

            @pl.when(full)
            def _():
                product(pl.ds(pl.multiple_of(slot * blk, blk), blk))

            @pl.when(jnp.logical_not(full))
            def _():
                product(pl.ds(pl.multiple_of(slot * blk + only * half, half), half))

            for h in range(2):
                for d in range(2):
                    @pl.when(jnp.logical_and(has(h, full, only), i == 0))
                    def _():
                        far_copy(j, d, h).start()

                    @pl.when(jnp.logical_and(has(h, full, only), i == 1 + d))
                    def _():
                        direct_copy(j, d, h).start()

            return 0

        lax.fori_loop(0, 4, one, 0)

    def gather_sent():
        def sent(sem):
            rc(own_part(0), own_part(0), sem, sem, partner).wait_send()

        for p in range(PARTS):
            sent(s1s.at[0, p])
            for k in range(4):
                for d in range(2):
                    sent(zs.at[d, 0, k, p])
                    sent(ps.at[1 + d, k, p])
                    if SIDE[k] == d:
                        sent(zs.at[d, 1, k, p])
                sent(ps.at[3, k, p])

        @pl.when(is_src)
        def _():
            for p in range(PARTS):
                for k in range(4):
                    sent(ps.at[0, k, p])
                    sent(zs.at[1 - SIDE[k], 1, k, p])

        @pl.when(not_src)
        def _():
            for p in range(PARTS):
                sent(s1s.at[1, p])
                for k in range(4):
                    sent(ps.at[4, k, p])

    def relayed(t):
        whole = jnp.where(t >= n_items - 2, n_items - 2, jnp.maximum(t - 1, 0))
        return jnp.where(t == HALVES, t, whole)

    def finished(t):
        return jnp.where(t >= n_items - 1, n_items - 4, jnp.where(t == n_items - 2, n_items - 5, 0))

    def step(t, _):
        lax.fori_loop(relayed(t - 1), relayed(t), relay_step, 0)
        lax.fori_loop(finished(t - 1), finished(t), final_step, 0)

        @pl.when(t == n_items - 1)
        def _():
            gather_sent()

        planes_ready(t)
        compute_step(t)
        gather_step(t)
        return 0

    lax.fori_loop(0, n_items, step, 0)
    lax.fori_loop(n_items - 2, n_items - 1, relay_step, 0)
    lax.fori_loop(n_items - 4, n_items - 3, final_step, 0)
    lax.fori_loop(n_items - 1, n_items, relay_step, 0)
    lax.fori_loop(n_items - 3, n_items, final_step, 0)

    def drain(j, _):
        w_copy(j).wait_send()
        for h in range(2):
            for d in range(2):
                far_copy(j, d, h).wait_send()
                direct_copy(j, d, h).wait_send()
                relay_copy(j, d, h).wait_send()
        return 0

    lax.fori_loop(0, n_ch, drain, 0)


def local(grad_out, weight):
    tb, feat = grad_out.shape
    hidden = weight.shape[0]
    n_ch = hidden // CH
    blk = 4 * tb
    dma = pltpu.SemaphoreType.DMA
    vmem = pl.BlockSpec(memory_space=pltpu.VMEM)
    hbm = pl.BlockSpec(memory_space=pltpu.HBM)
    return pl.pallas_call(
        kernel,
        out_shape=jax.ShapeDtypeStruct((blk, hidden), jnp.bfloat16),
        in_specs=[hbm, hbm],
        out_specs=vmem,
        scratch_shapes=[
            pltpu.VMEM((tb, feat), jnp.bfloat16),
            pltpu.VMEM((hidden, feat), jnp.bfloat16),
            pltpu.VMEM((2, 4 * blk, feat), jnp.bfloat16),
            pltpu.VMEM((hidden, feat), jnp.bfloat16),
            pltpu.VMEM((n_ch, 4 * blk, CH), jnp.float32),
            pltpu.VMEM((2, n_ch, 2, tb, CH), jnp.float32),
            pltpu.VMEM((2, n_ch, 2, tb, CH), jnp.float32),
            pltpu.VMEM((2, n_ch, blk, CH), jnp.float32),
            dma((2,)),
            dma((2, PARTS)), dma((3, PARTS)),
            dma((2, 2, 4, PARTS)), dma((2, 2, 4, PARTS)),
            dma((5, 4, PARTS)), dma((5, 4, PARTS)),
            dma((n_ch,)), dma((n_ch,)),
            dma((2, n_ch, 2)), dma((2, n_ch, 2)),
            dma((2, n_ch, 2)), dma((2, n_ch, 2)),
            dma((2, n_ch, 2)), dma((2, n_ch, 2)),
        ],
        compiler_params=pltpu.CompilerParams(
            collective_id=0, has_side_effects=True, vmem_limit_bytes=63 * 1024 * 1024
        ),
    )(grad_out, weight)


def solution(mesh):
    spec = P("col", "row")
    return jax.shard_map(local, mesh=mesh, in_specs=(spec, spec), out_specs=P("row", "col"), check_vma=False)
```

time: 75.6 us -> 72.2 us (0.955)
  the two profiles are of different devices: /device:TPU:20 before, /device:TPU:1 now
where the time goes in v4:
time: 72.2 us; the launch traced here: 71.9 us
  Pallas kernels  70 us (97%)
  local copies, waits for them, and re-layouts  1.82 us (3%)
    pallas_call x1, Pallas kernels, local(): pl.pallas_call(kernel, out_shape=jax.ShapeDtypeStruct((blk, hidden), jnp....  70 us
    unnamed x1, local copies, waits for them, and re-layouts  1.82 us

profile of v4, /device:TPU:1, one launch (start us, length us, event | category | flops | bytes accessed | tf_op | source)
XLA Modules:
  0.0 71.9 jit_solution(15554996915397479777)
XLA Ops:
  0.0 70.0 %shard_map.28 = bf16[256,896]{1,0:T(8,128)(2,1)} custom-call(bf16[64,1024]{1,0:T(8,128)(2,1)} %g_hbm.1, bf16[896,1024]{1,0:T(8,128)(2,1)} %w_hbm.1), custom_call_target="tpu_custom_call" | custom-call | tf_op jit(solution)/shard_map/pallas_call | solution.py:384
  70.1 1.8 %copy.4 = bf16[256,896]{1,0:T(8,128)(2,1)} copy(bf16[256,896]{1,0:T(8,128)(2,1)} %shard_map.28) | data formatting | bytes 917504

commit v5 on v4

--- a/solution.py
+++ b/solution.py
@@ -8,9 +8,11 @@
 MESH = pl.DeviceIdType.MESH
 CH = 128
 PARTS = 2
-ORDER = ((0, 0), (0, 1), (1, 0), (1, 1), (3, 0), (2, 0), (3, 1), (2, 1))
+FIRST = tuple((k, p) for k in (0, 1) for p in range(PARTS))
+ORDER = FIRST + tuple((k, p) for p in range(PARTS) for k in (3, 2))
 SIDE = (0, 1, 1, 0)
 HALVES = 4
+PAIRS = (0, 4, 6, 8)
 NT = (((1,), (1,)), ((), ()))
 
 
@@ -167,7 +169,7 @@
     @pl.when(is_src)
     def _():
         gbuf[0, pl.ds(pl.multiple_of(s0 * blk + (hi * 2 + c) * tb, tb), tb), :] = g_ref[...]
-        for k, p in ORDER[2:]:
+        for k, p in ORDER[PARTS:]:
             own_one(k, p)
         for k, p in ORDER:
             src_near_one(k, p)
@@ -178,7 +180,7 @@
     def _():
         for k, p in ORDER:
             mid_near_one(k, p)
-        for k, p in ORDER[:4]:
+        for k, p in FIRST:
             mid_far_one(k, p)
 
     def gather_step(t):
@@ -187,11 +189,12 @@
             for p in range(PARTS):
                 opp_one(3, 2, p)
 
-        for p, when in ((0, 0), (1, 1)):
+        for when in range(2):
             @pl.when(jnp.logical_and(not_src, t == when))
             def _():
-                for i in range(2):
-                    mid_far_one(3 - i, p)
+                for p in range(when * PARTS // 2, (when + 1) * PARTS // 2):
+                    for k in (3, 2):
+                        mid_far_one(k, p)
 
     def planes_ready(t):
         for when, ks in ((0, (0, 1)), (HALVES, (3, 2))):
@@ -270,42 +273,57 @@
 
     def compute_step(t):
         full, j, only = group_of(t)
-
-        @pl.when(jnp.logical_or(full, t < HALVES))
+        paired = sum((t == i).astype(jnp.int32) for i in PAIRS) > 0
+
+        after = sum((t == i + 1).astype(jnp.int32) for i in PAIRS)
+
+        @pl.when(jnp.logical_and(after == 0, jnp.logical_or(full, t < HALVES)))
         def _():
             w_copy(j).wait_recv()
 
-        at = pl.ds(pl.multiple_of(j * CH, CH), CH)
-
-        def product(rows):
+            @pl.when(paired)
+            def _():
+                w_copy(j + 1).wait_recv()
+
+        def product(rows, wide):
+            at = pl.ds(pl.multiple_of(j * CH, CH), wide * CH)
             total = lax.dot_general(gbuf[0, rows, :], w_ref[at, :], NT, preferred_element_type=jnp.float32)
             total += lax.dot_general(gbuf[1, rows, :], wn[at, :], NT, preferred_element_type=jnp.float32)
-            cbuf[j, rows, :] = total
+            for i in range(wide):
+                cbuf[j + i, rows, :] = total[:, i * CH : (i + 1) * CH]
 
         def one(i, _):
             slot = jnp.where(i < 2, jnp.where(i == 0, order[0], order[1]), jnp.where(i == 2, order[2], order[3]))
-
-            @pl.when(full)
-            def _():
-                product(pl.ds(pl.multiple_of(slot * blk, blk), blk))
-
-            @pl.when(jnp.logical_not(full))
-            def _():
-                product(pl.ds(pl.multiple_of(slot * blk + only * half, half), half))
-
-            for h in range(2):
-                for d in range(2):
-                    @pl.when(jnp.logical_and(has(h, full, only), i == 0))
-                    def _():
-                        far_copy(j, d, h).start()
-
-                    @pl.when(jnp.logical_and(has(h, full, only), i == 1 + d))
-                    def _():
-                        direct_copy(j, d, h).start()
-
+            for wide in (1, 2):
+                this = paired if wide == 2 else jnp.logical_not(paired)
+
+                @pl.when(jnp.logical_and(this, full))
+                def _():
+                    product(pl.ds(pl.multiple_of(slot * blk, blk), blk), wide)
+
+                @pl.when(jnp.logical_and(this, jnp.logical_not(full)))
+                def _():
+                    product(pl.ds(pl.multiple_of(slot * blk + only * half, half), half), wide)
+
+            def send(n, _):
+                for h in range(2):
+                    for d in range(2):
+                        @pl.when(jnp.logical_and(has(h, full, only), i == 0))
+                        def _():
+                            far_copy(j + n, d, h).start()
+
+                        @pl.when(jnp.logical_and(has(h, full, only), i == 1 + d))
+                        def _():
+                            direct_copy(j + n, d, h).start()
+
+                return 0
+
+            lax.fori_loop(0, jnp.where(paired, 2, 1), send, 0)
             return 0
 
-        lax.fori_loop(0, 4, one, 0)
+        @pl.when(after == 0)
+        def _():
+            lax.fori_loop(0, 4, one, 0)
 
     def gather_sent():
         def sent(sem):
@@ -336,30 +354,10 @@
                     sent(ps.at[4, k, p])
 
     def relayed(t):
-        whole = jnp.where(t >= n_items - 2, n_items - 2, jnp.maximum(t - 1, 0))
-        return jnp.where(t == HALVES, t, whole)
+        return jnp.clip(t - 2, 0, n_items - 3)
 
     def finished(t):
-        return jnp.where(t >= n_items - 1, n_items - 4, jnp.where(t == n_items - 2, n_items - 5, 0))
-
-    def step(t, _):
-        lax.fori_loop(relayed(t - 1), relayed(t), relay_step, 0)
-        lax.fori_loop(finished(t - 1), finished(t), final_step, 0)
-
-        @pl.when(t == n_items - 1)
-        def _():
-            gather_sent()
-
-        planes_ready(t)
-        compute_step(t)
-        gather_step(t)
-        return 0
-
-    lax.fori_loop(0, n_items, step, 0)
-    lax.fori_loop(n_items - 2, n_items - 1, relay_step, 0)
-    lax.fori_loop(n_items - 4, n_items - 3, final_step, 0)
-    lax.fori_loop(n_items - 1, n_items, relay_step, 0)
-    lax.fori_loop(n_items - 3, n_items, final_step, 0)
+        return jnp.where(t >= n_items - 2, n_items - 6, 0)
 
     def drain(j, _):
         w_copy(j).wait_send()
@@ -370,7 +368,23 @@
                 relay_copy(j, d, h).wait_send()
         return 0
 
-    lax.fori_loop(0, n_ch, drain, 0)
+    def step(t, _):
+        lax.fori_loop(relayed(t - 1), relayed(t), relay_step, 0)
+        lax.fori_loop(finished(t - 1), finished(t), final_step, 0)
+
+        planes_ready(t)
+        compute_step(t)
+        gather_step(t)
+        return 0
+
+    lax.fori_loop(0, n_items, step, 0)
+    lax.fori_loop(n_items - 3, n_items - 2, relay_step, 0)
+    lax.fori_loop(n_items - 6, n_items - 4, final_step, 0)
+    lax.fori_loop(n_items - 2, n_items, relay_step, 0)
+    gather_sent()
+    lax.fori_loop(0, n_ch - 3, drain, 0)
+    lax.fori_loop(n_items - 4, n_items, final_step, 0)
+    lax.fori_loop(n_ch - 3, n_ch, drain, 0)
 
 
 def local(grad_out, weight):

time: 72.2 us -> 70.6 us (0.978)
  Pallas kernels: 70 us -> 68.6 us
    pallas_call x1, Pallas kernels: 70 us -> 68.6 us  [local(): pl.pallas_call(kernel, out_shape=jax.ShapeDtypeStruct((blk, hidden), jnp....]
where the time goes in v5:
time: 70.6 us; the launch traced here: 70.4 us
  Pallas kernels  68.6 us (97%)
  local copies, waits for them, and re-layouts  1.82 us (3%)
    pallas_call x1, Pallas kernels, local(): pl.pallas_call(kernel, out_shape=jax.ShapeDtypeStruct((blk, hidden), jnp....  68.6 us
    unnamed x1, local copies, waits for them, and re-layouts  1.82 us

profile of v5, /device:TPU:1, one launch (start us, length us, event | category | flops | bytes accessed | tf_op | source)
XLA Modules:
  0.0 70.4 jit_solution(11747245327795776078)
XLA Ops:
  0.0 68.6 %shard_map.28 = bf16[256,896]{1,0:T(8,128)(2,1)} custom-call(bf16[64,1024]{1,0:T(8,128)(2,1)} %g_hbm.1, bf16[896,1024]{1,0:T(8,128)(2,1)} %w_hbm.1), custom_call_target="tpu_custom_call" | custom-call | tf_op jit(solution)/shard_map/pallas_call | solution.py:398
  68.6 1.8 %copy.4 = bf16[256,896]{1,0:T(8,128)(2,1)} copy(bf16[256,896]{1,0:T(8,128)(2,1)} %shard_map.28) | data formatting | bytes 917504

commit v6 on v5

--- a/solution.py
+++ b/solution.py
@@ -357,7 +357,7 @@
         return jnp.clip(t - 2, 0, n_items - 3)
 
     def finished(t):
-        return jnp.where(t >= n_items - 2, n_items - 6, 0)
+        return jnp.where(t >= n_items - 2, n_items - 8, 0)
 
     def drain(j, _):
         w_copy(j).wait_send()
@@ -378,12 +378,12 @@
         return 0
 
     lax.fori_loop(0, n_items, step, 0)
-    lax.fori_loop(n_items - 3, n_items - 2, relay_step, 0)
-    lax.fori_loop(n_items - 6, n_items - 4, final_step, 0)
-    lax.fori_loop(n_items - 2, n_items, relay_step, 0)
+    lax.fori_loop(n_items - 3, n_items - 1, relay_step, 0)
+    lax.fori_loop(n_items - 8, n_items - 6, final_step, 0)
+    lax.fori_loop(n_items - 1, n_items, relay_step, 0)
     gather_sent()
     lax.fori_loop(0, n_ch - 3, drain, 0)
-    lax.fori_loop(n_items - 4, n_items, final_step, 0)
+    lax.fori_loop(n_items - 6, n_items, final_step, 0)
     lax.fori_loop(n_ch - 3, n_ch, drain, 0)
 
 

time: 70.6 us -> 70.6 us (level)
  no operation moved by 1% of the time
where the time goes in v6:
time: 70.6 us; the launch traced here: 70.4 us
  Pallas kernels  68.6 us (97%)
  local copies, waits for them, and re-layouts  1.82 us (3%)
    pallas_call x1, Pallas kernels, local(): pl.pallas_call(kernel, out_shape=jax.ShapeDtypeStruct((blk, hidden), jnp....  68.6 us
    unnamed x1, local copies, waits for them, and re-layouts  1.82 us

profile of v6, /device:TPU:1, one launch (start us, length us, event | category | flops | bytes accessed | tf_op | source)
XLA Modules:
  0.0 70.4 jit_solution(12534729533784736228)
XLA Ops:
  0.0 68.6 %shard_map.28 = bf16[256,896]{1,0:T(8,128)(2,1)} custom-call(bf16[64,1024]{1,0:T(8,128)(2,1)} %g_hbm.1, bf16[896,1024]{1,0:T(8,128)(2,1)} %w_hbm.1), custom_call_target="tpu_custom_call" | custom-call | tf_op jit(solution)/shard_map/pallas_call | solution.py:398
  68.6 1.8 %copy.4 = bf16[256,896]{1,0:T(8,128)(2,1)} copy(bf16[256,896]{1,0:T(8,128)(2,1)} %shard_map.28) | data formatting | bytes 917504

commit v7 on v6

--- a/solution.py
+++ b/solution.py
@@ -46,16 +46,15 @@
     h_dev = dev(hi=1 - hi)
     wh_dev = dev(lo=1 - lo, hi=1 - hi)
 
+    g_in = pltpu.make_async_copy(g_hbm, g_ref, ls.at[0])
+    g_in.start()
     barrier = pltpu.get_barrier_semaphore()
     peers = (partner, *z_dev, *x_dev, w_dev, h_dev, wh_dev)
     for peer in peers:
         pl.semaphore_signal(barrier, inc=1, device_id=peer, device_id_type=MESH)
-    g_in = pltpu.make_async_copy(g_hbm, g_ref, ls.at[0])
     w_in = pltpu.make_async_copy(w_hbm, w_ref, ls.at[1])
-    g_in.start()
     w_in.start()
     g_in.wait()
-    w_in.wait()
     pl.semaphore_wait(barrier, len(peers))
 
     def rc(src, dst, ss, sr, to):
@@ -103,6 +102,7 @@
         at = pl.ds(pl.multiple_of(j * CH, CH), CH)
         return rc(w_ref.at[at, :], wn.at[at, :], ws.at[j], wr.at[j], w_dev)
 
+    w_in.wait()
     for j in range(n_ch):
         w_copy(j).start()
 

time: 70.6 us -> 70.6 us (level)
  no operation moved by 1% of the time
where the time goes in v7:
time: 70.6 us; the launch traced here: 70.4 us
  Pallas kernels  68.6 us (97%)
  local copies, waits for them, and re-layouts  1.82 us (3%)
    pallas_call x1, Pallas kernels, local(): pl.pallas_call(kernel, out_shape=jax.ShapeDtypeStruct((blk, hidden), jnp....  68.6 us
    unnamed x1, local copies, waits for them, and re-layouts  1.82 us

profile of v7, /device:TPU:1, one launch (start us, length us, event | category | flops | bytes accessed | tf_op | source)
XLA Modules:
  0.0 70.4 jit_solution(11631482237057234071)
XLA Ops:
  0.0 68.6 %shard_map.28 = bf16[256,896]{1,0:T(8,128)(2,1)} custom-call(bf16[64,1024]{1,0:T(8,128)(2,1)} %g_hbm.1, bf16[896,1024]{1,0:T(8,128)(2,1)} %w_hbm.1), custom_call_target="tpu_custom_call" | custom-call | tf_op jit(solution)/shard_map/pallas_call | solution.py:398
  68.6 1.8 %copy.4 = bf16[256,896]{1,0:T(8,128)(2,1)} copy(bf16[256,896]{1,0:T(8,128)(2,1)} %shard_map.28) | data formatting | bytes 917504

commit v8 on v6

--- a/solution.py
+++ b/solution.py
@@ -95,9 +95,9 @@
     @pl.when(not_src)
     def _():
         for p in range(PARTS):
-            there = place(s0, 1, hi, c, p)
-            rc(own_part(p), there, s1s.at[0, p], s1r.at[0, p], w_dev).start()
-            rc(own_part(p), there, s1s.at[1, p], s1r.at[1, p], wh_dev).start()
+            rc(own_part(p), place(s0, 1, hi, c, p), s1s.at[0, p], s1r.at[0, p], w_dev).start()
+        for p in range(PARTS):
+            rc(own_part(p), place(s0, 1, hi, c, p), s1s.at[1, p], s1r.at[1, p], wh_dev).start()
 
     def w_copy(j):
         at = pl.ds(pl.multiple_of(j * CH, CH), CH)

time: 70.6 us -> 70.6 us (level)
  no operation moved by 1% of the time
where the time goes in v8:
time: 70.6 us; the launch traced here: 70.4 us
  Pallas kernels  68.6 us (97%)
  local copies, waits for them, and re-layouts  1.82 us (3%)
    pallas_call x1, Pallas kernels, local(): pl.pallas_call(kernel, out_shape=jax.ShapeDtypeStruct((blk, hidden), jnp....  68.6 us
    unnamed x1, local copies, waits for them, and re-layouts  1.82 us

profile of v8, /device:TPU:1, one launch (start us, length us, event | category | flops | bytes accessed | tf_op | source)
XLA Modules:
  0.0 70.4 jit_solution(18251449818400887211)
XLA Ops:
  0.0 68.6 %shard_map.28 = bf16[256,896]{1,0:T(8,128)(2,1)} custom-call(bf16[64,1024]{1,0:T(8,128)(2,1)} %g_hbm.1, bf16[896,1024]{1,0:T(8,128)(2,1)} %w_hbm.1), custom_call_target="tpu_custom_call" | custom-call | tf_op jit(solution)/shard_map/pallas_call | solution.py:398
  68.6 1.8 %copy.4 = bf16[256,896]{1,0:T(8,128)(2,1)} copy(bf16[256,896]{1,0:T(8,128)(2,1)} %shard_map.28) | data formatting | bytes 917504
